TPU v7x, 32 devices: a whole 2x2x4 slice. The times are simulated.
32 devices in a mesh: pair: 4 (over y, x), aux: 8 (over z, core).
Axes of the slice: x: 2, y: 2, z: 4, core: 2. Of those that a mesh axis runs over, the one named last changes fastest.
Arguments:
- same_panels: bfloat16 [32, 2, 112, 59904], P('aux', None, None, 'pair'), may hold values from -1 to 1
- opposite_panels: bfloat16 [32, 2, 112, 59904], P('aux', None, None, 'pair'), may hold values from -1 to 1
- same_amplitudes: bfloat16 [32, 112, 112], replicated, may hold values from -2 to 2
- opposite_amplitudes: bfloat16 [32, 112, 112], replicated, may hold values from -2 to 2
- same_energies: float32 [32, 2, 112], replicated, may hold values from 0.5 to 3
- opposite_energies: float32 [32, 2, 112], replicated, may hold values from 0.5 to 3
- same_ranks: int32 [32], replicated, may hold values from 48 to 112
- opposite_ranks: int32 [32], replicated, may hold values from 48 to 112
Outputs:
- same_residual: float32 [32, 112, 112], P('pair', 'aux')
- opposite_residual: float32 [32, 112, 112], P('pair', 'aux')
Inputs may be any that keep to these rules, and one draw needn't show every extreme that they name: `same_ranks`: slots at or beyond a pair's rank are padding. `opposite_ranks`: slots at or beyond a pair's rank are padding.
All inputs are finite; a program needn't handle non-finite values.
Results may differ from a plain program's by a relative error of at most 0.0013.
Values may be sent and summed in bfloat16 or wider, within the bound.
No kernel may reach another device: no remote copies, remote signals or barrier semaphores. Data moves between devices by JAX's collectives and lax.ppermute only.
A program may use at most 128 MiB of HBM per device.

v0:
```python
import jax
import jax.numpy as jnp
from jax import lax
from jax.sharding import PartitionSpec as P


def slot_mask(ranks, slots):
    places = jnp.arange(slots, dtype=jnp.int32)
    return (places[None, :] < ranks[:, None]).astype(jnp.float32)


def masked_amplitudes(amplitudes, keep):
    outer = keep[:, :, None] * keep[:, None, :]
    return (amplitudes.astype(jnp.float32) * outer).astype(jnp.bfloat16)


def dressing_total(panels, masked):
    mixed = jnp.einsum("pab,pbn->pan", masked, panels[:, 1], preferred_element_type=jnp.float32)
    return jnp.sum(panels[:, 0].astype(jnp.float32) * mixed, axis=(0, 1))


def partial_terms(panels, coupling):
    exchange = jnp.einsum(
        "pan,pbn->pab", panels[:, 0], panels[:, 1], preferred_element_type=jnp.float32
    )
    scaled = (panels[:, 0].astype(jnp.float32) * coupling[None, None, :]).astype(jnp.bfloat16)
    coulomb = jnp.einsum("pan,pbn->pab", scaled, panels[:, 1], preferred_element_type=jnp.float32)
    return exchange + coulomb


def finish_rows(summed, amplitudes, energies, ranks, pair_start, row_start):
    count = summed.shape[0]
    rows = summed.shape[1]
    slots = amplitudes.shape[1]
    keep = slot_mask(lax.dynamic_slice_in_dim(ranks, pair_start, count, 0), slots)
    amplitude = lax.dynamic_slice_in_dim(amplitudes, pair_start, count, 0)
    masked = masked_amplitudes(amplitude, keep)
    masked_rows = lax.dynamic_slice_in_dim(masked, row_start, rows, 1).astype(jnp.float32)
    energy = lax.dynamic_slice_in_dim(energies, pair_start, count, 0)
    first_gap = lax.dynamic_slice_in_dim(energy[:, 0], row_start, rows, 1)
    keep_rows = lax.dynamic_slice_in_dim(keep, row_start, rows, 1)
    diagonal = (first_gap[:, :, None] + energy[:, 1][:, None, :]) * masked_rows
    return (summed + diagonal) * (keep_rows[:, :, None] * keep[:, None, :])


def local_masked(amplitudes, ranks, start, count):
    slots = amplitudes.shape[1]
    keep = slot_mask(lax.dynamic_slice_in_dim(ranks, start, count, 0), slots)
    return masked_amplitudes(lax.dynamic_slice_in_dim(amplitudes, start, count, 0), keep)


def body(
    same_panels,
    opposite_panels,
    same_amplitudes,
    opposite_amplitudes,
    same_energies,
    opposite_energies,
    same_ranks,
    opposite_ranks,
):
    block_count = same_panels.shape[0]
    pair_index = lax.axis_index("pair")
    aux_index = lax.axis_index("aux")
    owned = block_count * lax.axis_size("aux") // lax.axis_size("pair")
    rows = same_amplitudes.shape[1] // lax.axis_size("aux")
    start = aux_index * block_count
    same_masked = local_masked(same_amplitudes, same_ranks, start, block_count)
    opposite_masked = local_masked(opposite_amplitudes, opposite_ranks, start, block_count)
    partial_coupling = dressing_total(same_panels, same_masked) + dressing_total(
        opposite_panels, opposite_masked
    )
    coupling = lax.psum(partial_coupling, "aux")
    same_rows, opposite_rows = (
        lax.all_to_all(
            partial_terms(same_panels, coupling), "aux", split_axis=1, concat_axis=0, tiled=True
        ),
        lax.all_to_all(
            partial_terms(opposite_panels, coupling), "aux", split_axis=1, concat_axis=0, tiled=True
        ),
    )
    same_sum, opposite_sum = (
        lax.psum_scatter(same_rows, "pair", scatter_dimension=0, tiled=True),
        lax.psum_scatter(opposite_rows, "pair", scatter_dimension=0, tiled=True),
    )
    pair_start = pair_index * owned
    row_start = aux_index * rows
    same_residual = finish_rows(
        same_sum, same_amplitudes, same_energies, same_ranks, pair_start, row_start
    )
    opposite_residual = finish_rows(
        opposite_sum, opposite_amplitudes, opposite_energies, opposite_ranks, pair_start, row_start
    )
    return (same_residual, opposite_residual)


def solution(mesh):
    placed = (
        P("aux", None, None, "pair"),
        P("aux", None, None, "pair"),
        P(),
        P(),
        P(),
        P(),
        P(),
        P(),
    )
    return jax.shard_map(
        body,
        mesh=mesh,
        in_specs=placed,
        out_specs=(P("pair", "aux", None), P("pair", "aux", None)),
        check_vma=False,
    )
```

profile of v0, /device:TPU:0, one launch (start us, length us, event | category | flops | bytes accessed | tf_op | source)
XLA Modules:
  0.0 178.4 jit_solution(11435442703354790816)
XLA Ops:
  7.2 0.7 dynamic_slice.49
  7.9 0.1 fusion.52
  8.0 0.7 dynamic_slice.51
  8.7 0.1 fusion.53
  8.8 10.7 %fusion = f32[14976]{0:T(1024)S(1)} fusion(bf16[4,2,112,14976]{3,2,1,0:T(8,128)(2,1)} %param.8, f32[4,112]{1,0:T(4,128)S(1)} %fusion.52, bf16[32,112,112]{2,1,0:T(8,128)(2,1)} %param.10, s32[]{:T(128)S(6)} %select_n.6), kind=kOutput, calls=%fused_computation.4 | convolution fusion | flops 1523185024 | bytes 27015684 | tf_op jit(solution)/shard_map/pab,pbn->pan/dot_general | solution.py:18
  19.5 10.8 %fusion.2 = f32[14976]{0:T(1024)S(1)} fusion(bf16[4,2,112,14976]{3,2,1,0:T(8,128)(2,1)} %param.9, f32[4,112]{1,0:T(4,128)S(1)} %fusion.53, bf16[32,112,112]{2,1,0:T(8,128)(2,1)} %param.11, s32[]{:T(128)S(6)} %select_n.6), kind=kOutput, calls=%fused_computation.6 | convolution fusion | flops 1523185024 | bytes 27015684 | tf_op jit(solution)/shard_map/pab,pbn->pan/dot_general | solution.py:18
  30.3 30.8 %psum.7 = f32[14976]{0:T(1024)S(1)} all-reduce(f32[14976]{0:T(1024)S(1)} %add.78), channel_id=1, replica_groups=mesh['pair'=4,'aux'=8] {'aux'}, use_global_device_ids=true, to_apply=%region_2.0 | all-reduce | flops 14976 | bytes 119808 | tf_op jit(solution)/shard_map/psum | solution.py:73
  61.1 10.6 %fusion.6 = f32[4,112,112]{2,1,0:T(8,128)S(1)} fusion(f32[14976]{0:T(1024)S(1)} %psum.7, bf16[4,2,112,14976]{3,2,1,0:T(8,128)(2,1)} %param.8), kind=kOutput, calls=%fused_computation.9 | convolution fusion | flops 1522999296 | bytes 27097600 | tf_op jit(solution)/shard_map/pan,pbn->pab/dot_general | solution.py:27
  71.7 10.6 %fusion.32 = f32[4,112,112]{2,1,0:T(8,128)S(1)} fusion(f32[4,112,112]{2,1,0:T(8,128)S(1)} %fusion.6, bf16[4,2,112,14976]{3,2,1,0:T(8,128)(2,1)} %param.8), kind=kOutput, calls=%fused_computation.34 | convolution fusion | flops 1502921728 | bytes 27238400 | tf_op jit(solution)/shard_map/pan,pbn->pab/dot_general | solution.py:23
  82.3 0.0 copy-start
  82.3 0.8 copy.64
  83.1 3.6 %all-to-all-start = ((f32[4,112,112]{2,0,1:T(4,128)}), f32[4,112,112]{2,0,1:T(4,128)S(1)}, u32[]{:S(2)}, u32[]{:S(2)}) async-start(f32[4,112,112]{2,0,1:T(4,128)} %copy.64), calls=%async_computation | async-start | bytes 458752 | tf_op jit(solution)/shard_map/all_to_all | solution.py:75
  86.7 10.6 %fusion.4 = f32[4,112,112]{2,1,0:T(8,128)S(1)} fusion(f32[14976]{0:T(1024)S(1)} %psum.7, bf16[4,2,112,14976]{3,2,1,0:T(8,128)(2,1)} %param.9), kind=kOutput, calls=%fused_computation.8 | convolution fusion | flops 1522999296 | bytes 27097600 | tf_op jit(solution)/shard_map/pan,pbn->pab/dot_general | solution.py:27
  97.3 0.0 copy-start.1
  97.3 0.0 copy-done
  97.3 0.1 dynamic_slice.55
  97.4 0.1 fusion.48
  97.5 10.6 %fusion.37 = f32[4,112,112]{2,1,0:T(8,128)S(1)} fusion(f32[4,112,112]{2,1,0:T(8,128)S(1)} %fusion.4, bf16[4,2,112,14976]{3,2,1,0:T(8,128)(2,1)} %param.9), kind=kOutput, calls=%fused_computation.35 | convolution fusion | flops 1502921728 | bytes 27238400 | tf_op jit(solution)/shard_map/pan,pbn->pab/dot_general | solution.py:23
  108.1 0.1 constant_dynamic-slice_fusion.7
  108.2 0.7 constant_dynamic-slice_fusion.11
  108.9 0.0 copy-done.1
  108.9 0.1 dynamic_slice.61
  109.0 0.8 copy.71
  109.7 0.8 constant_dynamic-slice_fusion.5
  110.5 0.1 fusion.49
  110.6 0.0 all-to-all-done
  110.6 4.8 %all-to-all-start.1 = ((f32[4,112,112]{2,0,1:T(4,128)}), f32[4,112,112]{2,0,1:T(4,128)S(1)}, u32[]{:S(2)}, u32[]{:S(2)}) async-start(f32[4,112,112]{2,0,1:T(4,128)} %copy.71), calls=%async_computation.2 | async-start | bytes 458752 | tf_op jit(solution)/shard_map/all_to_all | solution.py:78
  115.4 0.0 reduce-scatter.3.cloned.1.call-start
  115.5 0.7 copy.65
  116.2 0.0 reduce-scatter.3.cloned.1.call-update
  116.2 0.0 reduce-scatter.5.cloned.1.call-start
  116.3 0.1 constant_dynamic-slice_fusion.2
  116.4 0.1 copy.76
  116.5 0.1 copy.69
  116.6 0.1 copy.70
  116.6 0.1 copy.67
  116.7 0.1 copy.77
  116.8 0.1 copy.74
  116.9 1.0 constant_dynamic-slice_fusion.4
  117.9 1.0 constant_dynamic-slice_fusion.9
  118.8 5.6 %all-to-all-done.1 = f32[4,112,112]{2,0,1:T(4,128)S(1)} async-done(((f32[4,112,112]{2,0,1:T(4,128)}), f32[4,112,112]{2,0,1:T(4,128)S(1)}, u32[]{:S(2)}, u32[]{:S(2)}) %all-to-all-start.1) | async-done | bytes 200736 | tf_op jit(solution)/shard_map/all_to_all | solution.py:78
  124.4 0.7 copy.72
  125.2 0.0 reduce-scatter.5.cloned.1.call-update
  125.2 0.7 constant_dynamic-slice_fusion.6
  125.9 17.9 %reduce-scatter.3.cloned.1.call-done = f32[8,14,112]{2,0,1:T(8,128)} async-done(((f32[32,14,112]{2,0,1:T(8,128)}), f32[8,14,112]{2,0,1:T(8,128)}) %reduce-scatter.3.cloned.1.call-update) | async-done | bytes 50192 | tf_op jit(solution)/shard_map/reduce_scatter | solution.py:83
  143.9 1.6 multiply_multiply_fusion.1
  145.4 24.6 %reduce-scatter.5.cloned.1.call-done = f32[8,14,112]{2,0,1:T(8,128)} async-done(((f32[32,14,112]{2,0,1:T(8,128)}), f32[8,14,112]{2,0,1:T(8,128)}) %reduce-scatter.5.cloned.1.call-update) | async-done | bytes 50192 | tf_op jit(solution)/shard_map/reduce_scatter | solution.py:84
  170.1 1.6 multiply_multiply_fusion
  (3 shorter events, 0.0 us)
Async XLA Ops:
  82.3 15.0 %copy-start = (s32[32]{0:T(128)S(1)}, s32[32]{0:T(128)}, u32[]{:S(2)}) copy-start(s32[32]{0:T(128)} %param.14) | copy-start | bytes 388
  83.1 27.5 %all-to-all-start = ((f32[4,112,112]{2,0,1:T(4,128)}), f32[4,112,112]{2,0,1:T(4,128)S(1)}, u32[]{:S(2)}, u32[]{:S(2)}) async-start(f32[4,112,112]{2,0,1:T(4,128)} %copy.64), calls=%async_computation | async-start | bytes 458752 | tf_op jit(solution)/shard_map/all_to_all | solution.py:75
  97.3 11.6 %copy-start.1 = (s32[32]{0:T(128)S(1)}, s32[32]{0:T(128)}, u32[]{:S(2)}) copy-start(s32[32]{0:T(128)} %param.15) | copy-start | bytes 388
  110.6 13.8 %all-to-all-start.1 = ((f32[4,112,112]{2,0,1:T(4,128)}), f32[4,112,112]{2,0,1:T(4,128)S(1)}, u32[]{:S(2)}, u32[]{:S(2)}) async-start(f32[4,112,112]{2,0,1:T(4,128)} %copy.71), calls=%async_computation.2 | async-start | bytes 458752 | tf_op jit(solution)/shard_map/all_to_all | solution.py:78
  115.4 28.4 %reduce-scatter.3.cloned.1.call-start = ((), (), s32[]{:S(2)}) async-start(), calls=%async_computation.4 | async-start | bytes 286720 | tf_op jit(solution)/shard_map/reduce_scatter | solution.py:83
  116.2 53.8 %reduce-scatter.5.cloned.1.call-start = ((), (), s32[]{:S(2)}) async-start(), calls=%async_computation.5 | async-start | bytes 286720 | tf_op jit(solution)/shard_map/reduce_scatter | solution.py:84
Sparse Core Ops, SparseCore 0:
  119.0 24.7 reduce-scatter.2
  146.7 23.3 reduce-scatter.4
where the time goes:
time: 179 us; the launch traced here: 178 us
  matrix products  63.9 us (36%)
  waiting for transfers between devices  48.2 us (27%)
  blocking collectives  30.8 us (17%)
  between operations  14.2 us (8%)
  local copies, waits for them, and re-layouts  9.48 us (5%)
  starting transfers between devices  8.49 us (5%)
  other arithmetic  3.41 us (2%)
    psum x1, blocking collectives, body(): coupling = lax.psum(partial_coupling, 'aux')  30.8 us
    reduce_scatter x1, waiting for transfers between devices, body(): lax.psum_scatter(opposite_rows, 'pair', scatter_dimension=0, tiled=True)  24.6 us
    dot_general x2, matrix products, dressing_total(): jnp.einsum('pab,pbn->pan', masked, panels[:, 1], preferred_element_type=j...  21.5 us
    dot_general x2, matrix products, partial_terms(): jnp.einsum('pan,pbn->pab', panels[:, 0], panels[:, 1], preferred_element_...  21.2 us
    dot_general x2, matrix products, partial_terms(): jnp.einsum('pan,pbn->pab', scaled, panels[:, 1], preferred_element_type=j...  21.2 us
    reduce_scatter x1, waiting for transfers between devices, body(): lax.psum_scatter(same_rows, 'pair', scatter_dimension=0, tiled=True)  17.9 us
    all_to_all x1, waiting for transfers between devices, body(): lax.all_to_all(partial_terms(opposite_panels, coupling), 'aux', split_axi...  5.62 us
    all_to_all x1, starting transfers between devices, body(): lax.all_to_all(partial_terms(opposite_panels, coupling), 'aux', split_axi...  4.83 us
  transfers between devices with their start and end apart: 4, of which 3 were waited for; matrix products, arithmetic and copies ran while one was open for 17% of the time, Pallas kernels for 0%

commit v1 on v0

--- a/solution.py
+++ b/solution.py
@@ -70,7 +70,8 @@
     partial_coupling = dressing_total(same_panels, same_masked) + dressing_total(
         opposite_panels, opposite_masked
     )
-    coupling = lax.psum(partial_coupling, "aux")
+    parts = lax.all_gather(partial_coupling, "aux", axis=0, tiled=False)
+    coupling = parts.sum(axis=0)
     same_rows, opposite_rows = (
         lax.all_to_all(
             partial_terms(same_panels, coupling), "aux", split_axis=1, concat_axis=0, tiled=True

time: 179 us -> 167 us (0.933)
  blocking collectives: 30.8 us -> 16.5 us
    psum x1 -> x0, blocking collectives: 30.8 us -> none  [body(): coupling = lax.psum(partial_coupling, 'aux')]
    all_gather x0 -> x1, blocking collectives: none -> 16.5 us  [body(): parts = lax.all_gather(partial_coupling, 'aux', axis=0, tiled=False)]
  transfers between devices with their start and end apart: 4 -> 4, of which waited for: 3 -> 3; matrix products, arithmetic and copies ran while one was open for 17% -> 18% of each run, Pallas kernels for 0% -> 0%
where the time goes in v1:
time: 167 us; the launch traced here: 166 us
  matrix products  63.9 us (38%)
  waiting for transfers between devices  48.2 us (29%)
  blocking collectives  16.5 us (10%)
  between operations  14.2 us (9%)
  starting transfers between devices  9.86 us (6%)
  local copies, waits for them, and re-layouts  9.53 us (6%)
  other arithmetic  3.76 us (2%)
    reduce_scatter x1, waiting for transfers between devices, body(): lax.psum_scatter(opposite_rows, 'pair', scatter_dimension=0, tiled=True)  24.6 us
    dot_general x2, matrix products, dressing_total(): jnp.einsum('pab,pbn->pan', masked, panels[:, 1], preferred_element_type=j...  21.5 us
    dot_general x2, matrix products, partial_terms(): jnp.einsum('pan,pbn->pab', scaled, panels[:, 1], preferred_element_type=j...  21.2 us
    dot_general x2, matrix products, partial_terms(): jnp.einsum('pan,pbn->pab', panels[:, 0], panels[:, 1], preferred_element_...  21.2 us
    reduce_scatter x1, waiting for transfers between devices, body(): lax.psum_scatter(same_rows, 'pair', scatter_dimension=0, tiled=True)  17.9 us
    all_gather x1, blocking collectives, body(): parts = lax.all_gather(partial_coupling, 'aux', axis=0, tiled=False)  16.5 us
    all_to_all x1, waiting for transfers between devices, body(): lax.all_to_all(partial_terms(opposite_panels, coupling), 'aux', split_axi...  5.62 us
    all_to_all x1, starting transfers between devices, body(): lax.all_to_all(partial_terms(opposite_panels, coupling), 'aux', split_axi...  5.08 us
  transfers between devices with their start and end apart: 4, of which 3 were waited for; matrix products, arithmetic and copies ran while one was open for 18% of the time, Pallas kernels for 0%

profile of v1, /device:TPU:0, one launch (start us, length us, event | category | flops | bytes accessed | tf_op | source)
XLA Modules:
  0.0 165.9 jit_solution(9484555093031298861)
XLA Ops:
  7.2 0.7 dynamic_slice.49
  7.9 0.1 fusion.52
  8.0 0.7 dynamic_slice.51
  8.7 0.1 fusion.53
  8.8 10.7 %fusion = f32[14976]{0:T(1024)S(1)} fusion(bf16[4,2,112,14976]{3,2,1,0:T(8,128)(2,1)} %param.8, f32[4,112]{1,0:T(4,128)S(1)} %fusion.52, bf16[32,112,112]{2,1,0:T(8,128)(2,1)} %param.10, s32[]{:T(128)S(6)} %select_n.6), kind=kOutput, calls=%fused_computation.4 | convolution fusion | flops 1523185024 | bytes 27015684 | tf_op jit(solution)/shard_map/pab,pbn->pan/dot_general | solution.py:18
  19.5 10.8 %fusion.2 = f32[14976]{0:T(1024)S(1)} fusion(bf16[4,2,112,14976]{3,2,1,0:T(8,128)(2,1)} %param.9, f32[4,112]{1,0:T(4,128)S(1)} %fusion.53, bf16[32,112,112]{2,1,0:T(8,128)(2,1)} %param.11, s32[]{:T(128)S(6)} %select_n.6), kind=kOutput, calls=%fused_computation.6 | convolution fusion | flops 1523185024 | bytes 27015684 | tf_op jit(solution)/shard_map/pab,pbn->pan/dot_general | solution.py:18
  30.4 16.5 %all-gather.1 = f32[8,1,14976]{2,1,0:T(1,128)S(1)} all-gather(f32[1,1,14976]{2,1,0:T(1,128)S(1)} %reshape.178), channel_id=2, replica_groups=mesh['pair'=4,'aux'=8] {'aux'}, dimensions={0}, use_global_device_ids=true | all-gather | bytes 539136 | tf_op jit(solution)/shard_map/all_gather | solution.py:73
  46.8 0.4 reduce_sum.29
  47.2 10.6 %fusion.6 = f32[4,112,112]{2,1,0:T(8,128)S(1)} fusion(f32[14976]{0:T(1024)S(1)} %reduce_sum.29, bf16[4,2,112,14976]{3,2,1,0:T(8,128)(2,1)} %param.8), kind=kOutput, calls=%fused_computation.9 | convolution fusion | flops 1522999296 | bytes 27097600 | tf_op jit(solution)/shard_map/pan,pbn->pab/dot_general | solution.py:27
  57.8 10.6 %fusion.32 = f32[4,112,112]{2,1,0:T(8,128)S(1)} fusion(f32[4,112,112]{2,1,0:T(8,128)S(1)} %fusion.6, bf16[4,2,112,14976]{3,2,1,0:T(8,128)(2,1)} %param.8), kind=kOutput, calls=%fused_computation.34 | convolution fusion | flops 1502921728 | bytes 27238400 | tf_op jit(solution)/shard_map/pan,pbn->pab/dot_general | solution.py:23
  68.4 0.0 copy-start
  68.4 0.8 copy.64
  69.2 4.7 %all-to-all-start = ((f32[4,112,112]{2,0,1:T(4,128)}), f32[4,112,112]{2,0,1:T(4,128)S(1)}, u32[]{:S(2)}, u32[]{:S(2)}) async-start(f32[4,112,112]{2,0,1:T(4,128)} %copy.64), calls=%async_computation | async-start | bytes 458752 | tf_op jit(solution)/shard_map/all_to_all | solution.py:76
  73.9 10.6 %fusion.4 = f32[4,112,112]{2,1,0:T(8,128)S(1)} fusion(f32[14976]{0:T(1024)S(1)} %reduce_sum.29, bf16[4,2,112,14976]{3,2,1,0:T(8,128)(2,1)} %param.9), kind=kOutput, calls=%fused_computation.8 | convolution fusion | flops 1522999296 | bytes 27097600 | tf_op jit(solution)/shard_map/pan,pbn->pab/dot_general | solution.py:27
  84.5 0.0 copy-start.1
  84.5 0.0 copy-done
  84.5 0.1 dynamic_slice.55
  84.6 0.1 fusion.48
  84.7 10.6 %fusion.37 = f32[4,112,112]{2,1,0:T(8,128)S(1)} fusion(f32[4,112,112]{2,1,0:T(8,128)S(1)} %fusion.4, bf16[4,2,112,14976]{3,2,1,0:T(8,128)(2,1)} %param.9), kind=kOutput, calls=%fused_computation.35 | convolution fusion | flops 1502921728 | bytes 27238400 | tf_op jit(solution)/shard_map/pan,pbn->pab/dot_general | solution.py:23
  95.3 0.1 constant_dynamic-slice_fusion.7
  95.4 0.7 constant_dynamic-slice_fusion.11
  96.1 0.1 dynamic_slice.61
  96.1 0.8 copy.71
  96.9 0.8 constant_dynamic-slice_fusion.5
  97.7 0.1 fusion.49
  97.8 0.0 all-to-all-done
  97.8 5.1 %all-to-all-start.1 = ((f32[4,112,112]{2,0,1:T(4,128)}), f32[4,112,112]{2,0,1:T(4,128)S(1)}, u32[]{:S(2)}, u32[]{:S(2)}) async-start(f32[4,112,112]{2,0,1:T(4,128)} %copy.71), calls=%async_computation.2 | async-start | bytes 458752 | tf_op jit(solution)/shard_map/all_to_all | solution.py:79
  102.9 0.0 reduce-scatter.3.cloned.1.call-start
  102.9 0.7 copy.65
  103.7 0.0 reduce-scatter.3.cloned.1.call-update
  103.7 0.0 reduce-scatter.5.cloned.1.call-start
  103.7 0.1 constant_dynamic-slice_fusion.2
  103.8 0.1 copy.76
  103.9 0.1 copy.69
  104.0 0.1 copy.70
  104.1 0.1 copy.67
  104.2 0.1 copy.77
  104.2 0.1 copy.74
  104.3 1.0 constant_dynamic-slice_fusion.4
  105.3 1.0 constant_dynamic-slice_fusion.9
  106.3 5.6 %all-to-all-done.1 = f32[4,112,112]{2,0,1:T(4,128)S(1)} async-done(((f32[4,112,112]{2,0,1:T(4,128)}), f32[4,112,112]{2,0,1:T(4,128)S(1)}, u32[]{:S(2)}, u32[]{:S(2)}) %all-to-all-start.1) | async-done | bytes 200736 | tf_op jit(solution)/shard_map/all_to_all | solution.py:79
  111.9 0.7 copy.72
  112.6 0.0 reduce-scatter.5.cloned.1.call-update
  112.7 0.7 constant_dynamic-slice_fusion.6
  113.4 17.9 %reduce-scatter.3.cloned.1.call-done = f32[8,14,112]{2,0,1:T(8,128)} async-done(((f32[32,14,112]{2,0,1:T(8,128)}), f32[8,14,112]{2,0,1:T(8,128)}) %reduce-scatter.3.cloned.1.call-update) | async-done | bytes 50192 | tf_op jit(solution)/shard_map/reduce_scatter | solution.py:84
  131.3 1.6 multiply_multiply_fusion.1
  132.9 24.6 %reduce-scatter.5.cloned.1.call-done = f32[8,14,112]{2,0,1:T(8,128)} async-done(((f32[32,14,112]{2,0,1:T(8,128)}), f32[8,14,112]{2,0,1:T(8,128)}) %reduce-scatter.5.cloned.1.call-update) | async-done | bytes 50192 | tf_op jit(solution)/shard_map/reduce_scatter | solution.py:85
  157.5 1.6 multiply_multiply_fusion
  (5 shorter events, 0.1 us)
Async XLA Ops:
  68.4 16.1 %copy-start = (s32[32]{0:T(128)S(1)}, s32[32]{0:T(128)}, u32[]{:S(2)}) copy-start(s32[32]{0:T(128)} %param.14) | copy-start | bytes 388
  69.2 28.6 %all-to-all-start = ((f32[4,112,112]{2,0,1:T(4,128)}), f32[4,112,112]{2,0,1:T(4,128)S(1)}, u32[]{:S(2)}, u32[]{:S(2)}) async-start(f32[4,112,112]{2,0,1:T(4,128)} %copy.64), calls=%async_computation | async-start | bytes 458752 | tf_op jit(solution)/shard_map/all_to_all | solution.py:76
  84.5 11.6 %copy-start.1 = (s32[32]{0:T(128)S(1)}, s32[32]{0:T(128)}, u32[]{:S(2)}) copy-start(s32[32]{0:T(128)} %param.15) | copy-start | bytes 388
  97.8 14.1 %all-to-all-start.1 = ((f32[4,112,112]{2,0,1:T(4,128)}), f32[4,112,112]{2,0,1:T(4,128)S(1)}, u32[]{:S(2)}, u32[]{:S(2)}) async-start(f32[4,112,112]{2,0,1:T(4,128)} %copy.71), calls=%async_computation.2 | async-start | bytes 458752 | tf_op jit(solution)/shard_map/all_to_all | solution.py:79
  102.9 28.5 %reduce-scatter.3.cloned.1.call-start = ((), (), s32[]{:S(2)}) async-start(), calls=%async_computation.4 | async-start | bytes 286720 | tf_op jit(solution)/shard_map/reduce_scatter | solution.py:84
  103.7 53.8 %reduce-scatter.5.cloned.1.call-start = ((), (), s32[]{:S(2)}) async-start(), calls=%async_computation.5 | async-start | bytes 286720 | tf_op jit(solution)/shard_map/reduce_scatter | solution.py:85
Sparse Core Ops, SparseCore 0:
  106.5 24.8 reduce-scatter.2
  134.1 23.3 reduce-scatter.4
